TPU v7x, 32 devices: a whole 2x2x4 slice. The times are simulated.
32 devices in a mesh: row: 4 (over x, core), col: 8 (over z, y).
Axes of the slice: x: 2, y: 2, z: 4, core: 2. Of those that a mesh axis runs over, the one named last changes fastest.
Arguments:
- x_rows: float32 [16, 16384], P(None, ('row', 'col')), may hold values from -6 to 6
- alpha_rows: float32 [16384], P(('row', 'col')), may hold values from -0.5 to 1.5
- x_cols: float32 [16, 8192], P(None, ('col', 'row')), may hold values from -6 to 6
- alpha_cols: float32 [8192], P(('col', 'row')), may hold values from -0.0073242188 to 0.021972656
- lengthscale: float32 [16], replicated, may hold values from 1.2 to 2.5
Outputs:
- row_terms: float32 [16, 16384], P(None, ('row', 'col'))
- kernel_alpha: float32 [16384], P(('row', 'col'))
- grad: float32 [16], replicated
All inputs are finite; a program needn't handle non-finite values.
Results may differ from a plain program's by a relative error of at most 0.00021.
Values sent between devices are 32-bit elements; how exact they have to be, the bound alone decides.
A program may use at most 64 MiB of HBM per device.

v0:
```python
import jax
import jax.numpy as jnp
from jax import lax
from jax.sharding import PartitionSpec as P


def fold_terms(partials, row_scaled, row_alpha):
    dims = row_scaled.shape[0]
    weight_sum = partials[0]
    first_moment = partials[1 : 1 + dims]
    second_moment = partials[1 + dims :]
    terms = (
        0.5
        * row_alpha[None, :]
        * (
            row_scaled * row_scaled * weight_sum[None, :]
            - 2.0 * row_scaled * first_moment
            + second_moment
        )
    )
    return (terms, weight_sum)


def on_device(x_rows, alpha_rows, x_cols, alpha_cols, lengthscale):
    dims = x_rows.shape[0]
    inverse_scale = 1.0 / lengthscale
    own_scaled = x_rows * inverse_scale[:, None]
    own_rows = jnp.concatenate([own_scaled, alpha_rows[None, :]], 0)
    gathered = lax.all_gather(own_rows, "col", axis=1, tiled=True)
    row_scaled = gathered[:dims]
    row_alpha = gathered[dims]
    row_count = row_scaled.shape[1]
    block_rows = min(512, row_count)
    block_count = row_count // block_rows
    row_norms = jnp.sum(row_scaled * row_scaled, 0)
    own_cols = jnp.concatenate([x_cols * inverse_scale[:, None], alpha_cols[None, :]], 0)
    empty = jnp.zeros((2 * dims + 1, row_count), jnp.float32)
    shard_piece = lax.all_gather(own_cols, "row", axis=1, tiled=True)
    col_scaled = shard_piece[:dims]
    col_alpha = shard_piece[dims]
    col_norms = jnp.sum(col_scaled * col_scaled, 0)
    values = jnp.concatenate(
        [
            col_alpha[None, :],
            col_alpha[None, :] * col_scaled,
            col_alpha[None, :] * col_scaled * col_scaled,
        ],
        0,
    )

    def add_block(block_index, carried):
        offset = block_index * block_rows
        row_block = lax.dynamic_slice_in_dim(row_scaled, offset, block_rows, 1)
        block_norms = lax.dynamic_slice_in_dim(row_norms, offset, block_rows, 0)
        cross = lax.dot_general(
            row_block,
            col_scaled,
            (((0,), (0,)), ((), ())),
            precision=lax.Precision.HIGHEST,
            preferred_element_type=jnp.float32,
        )
        kernel = jnp.exp(-0.5 * (block_norms[:, None] + col_norms[None, :] - 2.0 * cross))
        contrib = lax.dot_general(
            values,
            kernel,
            (((1,), (1,)), ((), ())),
            precision=lax.Precision.HIGHEST,
            preferred_element_type=jnp.float32,
        )
        earlier = lax.dynamic_slice_in_dim(carried, offset, block_rows, 1)
        return lax.dynamic_update_slice_in_dim(carried, earlier + contrib, offset, 1)

    partials = lax.fori_loop(0, block_count, add_block, empty)
    summed = lax.psum_scatter(partials, "col", scatter_dimension=1, tiled=True)
    row_terms, kernel_alpha = fold_terms(summed, own_scaled, alpha_rows)
    tile_terms, tile_sum = fold_terms(partials, row_scaled, row_alpha)
    total_rows = row_count * lax.axis_size("row")
    grad = lax.psum(jnp.sum(tile_terms, 1), ("row", "col")) / total_rows
    return (row_terms, kernel_alpha, grad)


def solution(mesh):
    return jax.shard_map(
        on_device,
        mesh=mesh,
        in_specs=(
            P(None, ("row", "col")),
            P(("row", "col")),
            P(None, ("col", "row")),
            P(("col", "row")),
            P(),
        ),
        out_specs=(P(None, ("row", "col")), P(("row", "col")), P()),
        check_vma=False,
    )
```

profile of v0, /device:TPU:0, one launch (start us, length us, event | category | flops | bytes accessed | tf_op | source)
XLA Modules:
  0.0 159.6 jit_solution(6759463865752624172)
XLA Ops:
  7.2 0.0 reduce-scatter.2.cloned.1.call-start
  7.2 0.7 broadcast_divide_fusion
  7.9 0.8 broadcast_multiply_fusion.2
  8.7 0.7 pad_maximum_fusion.2
  9.3 6.3 %all_gather.7 = f32[17,1024]{1,0:T(8,128)S(1)} all-gather(f32[17,256]{1,0:T(8,128)S(1)} %pad_maximum_fusion.2), channel_id=1, replica_groups=mesh['row'=4,'col'=8] {'row'}, dimensions={1}, use_global_device_ids=true | all-gather | bytes 87040 | tf_op jit(solution)/shard_map/all_gather | solution.py:38
  15.7 0.8 broadcast_multiply_fusion.1
  16.5 0.7 pad_maximum_fusion.1
  17.2 32.0 %all_gather.6 = f32[17,4096]{1,0:T(8,128)S(1)} all-gather(f32[17,512]{1,0:T(8,128)S(1)} %pad_maximum_fusion.1), channel_id=1, replica_groups=mesh['row'=4,'col'=8] {'col'}, dimensions={1}, use_global_device_ids=true | all-gather | bytes 313344 | tf_op jit(solution)/shard_map/all_gather | solution.py:29
  49.3 0.0 copy-start.3
  49.4 0.0 copy-start.1
  49.4 35.8 %while.13 = (s32[]{:T(128)}, f32[33,4096]{1,0:T(8,128)S(1)}, f32[4096]{0:T(1024)S(1)}, f32[1024]{0:T(1024)S(1)}, f32[16,4096]{1,0:T(8,128)S(1)}, /*index=5*/f32[...) while((s32[]{:T(128)}, f32[33,4096]{1,0:T(8,128)S(1)}, ...), condition=%wide.region_3.0_spmd, body=%wide.region_2.0_spmd.sunk | while | flops 310395392 | bytes 4630695 | solution.py:73
  49.4 1.8 %fusion.40 = f32[512,1024]{1,0:T(8,128)S(1)} fusion(f32[16,1024]{1,0:T(8,128)S(1)} %get-tuple-element.218, f32[16,4096]{1,0:T(8,128)S(1)} %get-tuple-element.217, s32[]{:T(128)S(6)} %select_n.11), kind=kOutput, calls=%fused_computation.13.clone.1 | convolution fusion | flops 100663296 | bytes 2195460 | tf_op jit(solution)/shard_map/while/body/eval_jaxpr/dot_general | solution.py:55
  51.2 0.1 dynamic_slice.29
  51.3 2.5 %fusion.41 = f32[33,4096]{1,0:T(8,128)S(1)} fusion(f32[33,4096]{1,0:T(8,128)S(1)} %get-tuple-element.203, s32[]{:T(128)S(6)} %select_n.11, f32[33,1024]{1,0:T(8,128)S(1)} %get-tuple-element.219, f32[512,1024]{1,0:T(8,128)S(1)} %fusion.40, f32[1024]{0:T(1024)S(1)} %get-tuple-element.216, f32[512]{0:T(512)S(1)} %dynamic_slice.29), kind=kOutput, calls=%fused_computation.8.clone.1 | convolution fusion | flops 209732096 | bytes 2430980 | tf_op jit(solution)/shard_map/while/body/eval_jaxpr/dot_general | solution.py:63
  53.9 1.8 %fusion.40 = f32[512,1024]{1,0:T(8,128)S(1)} fusion(f32[16,1024]{1,0:T(8,128)S(1)} %get-tuple-element.218, f32[16,4096]{1,0:T(8,128)S(1)} %get-tuple-element.217, s32[]{:T(128)S(6)} %select_n.11), kind=kOutput, calls=%fused_computation.13.clone.1 | convolution fusion | flops 100663296 | bytes 2195460 | tf_op jit(solution)/shard_map/while/body/eval_jaxpr/dot_general | solution.py:55
  55.7 0.1 dynamic_slice.29
  55.8 2.5 %fusion.41 = f32[33,4096]{1,0:T(8,128)S(1)} fusion(f32[33,4096]{1,0:T(8,128)S(1)} %get-tuple-element.203, s32[]{:T(128)S(6)} %select_n.11, f32[33,1024]{1,0:T(8,128)S(1)} %get-tuple-element.219, f32[512,1024]{1,0:T(8,128)S(1)} %fusion.40, f32[1024]{0:T(1024)S(1)} %get-tuple-element.216, f32[512]{0:T(512)S(1)} %dynamic_slice.29), kind=kOutput, calls=%fused_computation.8.clone.1 | convolution fusion | flops 209732096 | bytes 2430980 | tf_op jit(solution)/shard_map/while/body/eval_jaxpr/dot_general | solution.py:63
  58.3 1.8 %fusion.40 = f32[512,1024]{1,0:T(8,128)S(1)} fusion(f32[16,1024]{1,0:T(8,128)S(1)} %get-tuple-element.218, f32[16,4096]{1,0:T(8,128)S(1)} %get-tuple-element.217, s32[]{:T(128)S(6)} %select_n.11), kind=kOutput, calls=%fused_computation.13.clone.1 | convolution fusion | flops 100663296 | bytes 2195460 | tf_op jit(solution)/shard_map/while/body/eval_jaxpr/dot_general | solution.py:55
  60.2 0.1 dynamic_slice.29
  60.3 2.5 %fusion.41 = f32[33,4096]{1,0:T(8,128)S(1)} fusion(f32[33,4096]{1,0:T(8,128)S(1)} %get-tuple-element.203, s32[]{:T(128)S(6)} %select_n.11, f32[33,1024]{1,0:T(8,128)S(1)} %get-tuple-element.219, f32[512,1024]{1,0:T(8,128)S(1)} %fusion.40, f32[1024]{0:T(1024)S(1)} %get-tuple-element.216, f32[512]{0:T(512)S(1)} %dynamic_slice.29), kind=kOutput, calls=%fused_computation.8.clone.1 | convolution fusion | flops 209732096 | bytes 2430980 | tf_op jit(solution)/shard_map/while/body/eval_jaxpr/dot_general | solution.py:63
  62.8 1.8 %fusion.40 = f32[512,1024]{1,0:T(8,128)S(1)} fusion(f32[16,1024]{1,0:T(8,128)S(1)} %get-tuple-element.218, f32[16,4096]{1,0:T(8,128)S(1)} %get-tuple-element.217, s32[]{:T(128)S(6)} %select_n.11), kind=kOutput, calls=%fused_computation.13.clone.1 | convolution fusion | flops 100663296 | bytes 2195460 | tf_op jit(solution)/shard_map/while/body/eval_jaxpr/dot_general | solution.py:55
  64.6 0.1 dynamic_slice.29
  64.7 2.5 %fusion.41 = f32[33,4096]{1,0:T(8,128)S(1)} fusion(f32[33,4096]{1,0:T(8,128)S(1)} %get-tuple-element.203, s32[]{:T(128)S(6)} %select_n.11, f32[33,1024]{1,0:T(8,128)S(1)} %get-tuple-element.219, f32[512,1024]{1,0:T(8,128)S(1)} %fusion.40, f32[1024]{0:T(1024)S(1)} %get-tuple-element.216, f32[512]{0:T(512)S(1)} %dynamic_slice.29), kind=kOutput, calls=%fused_computation.8.clone.1 | convolution fusion | flops 209732096 | bytes 2430980 | tf_op jit(solution)/shard_map/while/body/eval_jaxpr/dot_general | solution.py:63
  67.3 1.8 %fusion.40 = f32[512,1024]{1,0:T(8,128)S(1)} fusion(f32[16,1024]{1,0:T(8,128)S(1)} %get-tuple-element.218, f32[16,4096]{1,0:T(8,128)S(1)} %get-tuple-element.217, s32[]{:T(128)S(6)} %select_n.11), kind=kOutput, calls=%fused_computation.13.clone.1 | convolution fusion | flops 100663296 | bytes 2195460 | tf_op jit(solution)/shard_map/while/body/eval_jaxpr/dot_general | solution.py:55
  69.1 0.1 dynamic_slice.29
  69.2 2.5 %fusion.41 = f32[33,4096]{1,0:T(8,128)S(1)} fusion(f32[33,4096]{1,0:T(8,128)S(1)} %get-tuple-element.203, s32[]{:T(128)S(6)} %select_n.11, f32[33,1024]{1,0:T(8,128)S(1)} %get-tuple-element.219, f32[512,1024]{1,0:T(8,128)S(1)} %fusion.40, f32[1024]{0:T(1024)S(1)} %get-tuple-element.216, f32[512]{0:T(512)S(1)} %dynamic_slice.29), kind=kOutput, calls=%fused_computation.8.clone.1 | convolution fusion | flops 209732096 | bytes 2430980 | tf_op jit(solution)/shard_map/while/body/eval_jaxpr/dot_general | solution.py:63
  71.7 1.8 %fusion.40 = f32[512,1024]{1,0:T(8,128)S(1)} fusion(f32[16,1024]{1,0:T(8,128)S(1)} %get-tuple-element.218, f32[16,4096]{1,0:T(8,128)S(1)} %get-tuple-element.217, s32[]{:T(128)S(6)} %select_n.11), kind=kOutput, calls=%fused_computation.13.clone.1 | convolution fusion | flops 100663296 | bytes 2195460 | tf_op jit(solution)/shard_map/while/body/eval_jaxpr/dot_general | solution.py:55
  73.6 0.1 dynamic_slice.29
  73.7 2.5 %fusion.41 = f32[33,4096]{1,0:T(8,128)S(1)} fusion(f32[33,4096]{1,0:T(8,128)S(1)} %get-tuple-element.203, s32[]{:T(128)S(6)} %select_n.11, f32[33,1024]{1,0:T(8,128)S(1)} %get-tuple-element.219, f32[512,1024]{1,0:T(8,128)S(1)} %fusion.40, f32[1024]{0:T(1024)S(1)} %get-tuple-element.216, f32[512]{0:T(512)S(1)} %dynamic_slice.29), kind=kOutput, calls=%fused_computation.8.clone.1 | convolution fusion | flops 209732096 | bytes 2430980 | tf_op jit(solution)/shard_map/while/body/eval_jaxpr/dot_general | solution.py:63
  76.2 1.8 %fusion.40 = f32[512,1024]{1,0:T(8,128)S(1)} fusion(f32[16,1024]{1,0:T(8,128)S(1)} %get-tuple-element.218, f32[16,4096]{1,0:T(8,128)S(1)} %get-tuple-element.217, s32[]{:T(128)S(6)} %select_n.11), kind=kOutput, calls=%fused_computation.13.clone.1 | convolution fusion | flops 100663296 | bytes 2195460 | tf_op jit(solution)/shard_map/while/body/eval_jaxpr/dot_general | solution.py:55
  78.1 0.1 dynamic_slice.29
  78.1 2.5 %fusion.41 = f32[33,4096]{1,0:T(8,128)S(1)} fusion(f32[33,4096]{1,0:T(8,128)S(1)} %get-tuple-element.203, s32[]{:T(128)S(6)} %select_n.11, f32[33,1024]{1,0:T(8,128)S(1)} %get-tuple-element.219, f32[512,1024]{1,0:T(8,128)S(1)} %fusion.40, f32[1024]{0:T(1024)S(1)} %get-tuple-element.216, f32[512]{0:T(512)S(1)} %dynamic_slice.29), kind=kOutput, calls=%fused_computation.8.clone.1 | convolution fusion | flops 209732096 | bytes 2430980 | tf_op jit(solution)/shard_map/while/body/eval_jaxpr/dot_general | solution.py:63
  80.7 1.8 %fusion.40 = f32[512,1024]{1,0:T(8,128)S(1)} fusion(f32[16,1024]{1,0:T(8,128)S(1)} %get-tuple-element.218, f32[16,4096]{1,0:T(8,128)S(1)} %get-tuple-element.217, s32[]{:T(128)S(6)} %select_n.11), kind=kOutput, calls=%fused_computation.13.clone.1 | convolution fusion | flops 100663296 | bytes 2195460 | tf_op jit(solution)/shard_map/while/body/eval_jaxpr/dot_general | solution.py:55
  82.5 0.1 dynamic_slice.29
  82.6 2.5 %fusion.41 = f32[33,4096]{1,0:T(8,128)S(1)} fusion(f32[33,4096]{1,0:T(8,128)S(1)} %get-tuple-element.203, s32[]{:T(128)S(6)} %select_n.11, f32[33,1024]{1,0:T(8,128)S(1)} %get-tuple-element.219, f32[512,1024]{1,0:T(8,128)S(1)} %fusion.40, f32[1024]{0:T(1024)S(1)} %get-tuple-element.216, f32[512]{0:T(512)S(1)} %dynamic_slice.29), kind=kOutput, calls=%fused_computation.8.clone.1 | convolution fusion | flops 209732096 | bytes 2430980 | tf_op jit(solution)/shard_map/while/body/eval_jaxpr/dot_general | solution.py:63
  85.2 0.0 copy-start
  85.2 0.8 copy-done
  86.0 0.0 reduce-scatter.2.cloned.1.call-update
  86.0 0.9 slice.37
  86.9 1.3 multiply_reduce_fusion
  88.3 39.4 %psum.7 = f32[16]{0:T(128)S(1)} all-reduce(f32[16]{0:T(128)S(1)} %multiply_reduce_fusion), channel_id=1, replica_groups=mesh['row'=4,'col'=8] {'row','col'}, use_global_device_ids=true, to_apply=%region_6.0 | all-reduce | flops 16 | bytes 128 | tf_op jit(solution)/shard_map/psum | solution.py:78
  127.7 0.5 broadcast_multiply_fusion.4
  128.2 0.0 copy-done.3
  128.2 22.2 %reduce-scatter.2.cloned.1.call-done = f32[33,512]{1,0:T(8,128)} async-done(((f32[33,4096]{1,0:T(8,128)}), f32[33,512]{1,0:T(8,128)}) %reduce-scatter.2.cloned.1.call-update) | async-done | bytes 67600 | tf_op jit(solution)/shard_map/reduce_scatter | solution.py:74
  150.4 0.7 slice.43
  151.2 0.0 copy-start.2
  151.2 0.0 copy-done.1
  151.2 1.6 fusion.24
  152.7 0.0 copy-done.2
  (7 shorter events, 0.2 us)
Async XLA Ops:
  7.2 143.3 %reduce-scatter.2.cloned.1.call-start = ((), (), s32[]{:S(2)}) async-start(), calls=%async_computation.1 | async-start | bytes 737280 | tf_op jit(solution)/shard_map/reduce_scatter | solution.py:74
  49.3 78.8 %copy-start.3 = (f32[512]{0:T(512)S(1)}, f32[512]{0:T(512)}, u32[]{:S(2)}) copy-start(f32[512]{0:T(512)} %param.8) | copy-start | bytes 6148
  49.4 101.8 %copy-start.1 = (f32[16,512]{1,0:T(8,128)S(1)}, f32[16,512]{1,0:T(8,128)}, u32[]{:S(2)}) copy-start(f32[16,512]{1,0:T(8,128)} %param.7) | copy-start | bytes 98308
  85.2 0.8 copy-start
  151.2 1.6 copy-start.2
Sparse Core Ops, SparseCore 0:
  86.1 64.2 reduce-scatter.1
where the time goes:
time: 160 us
  blocking collectives  77.7 us (49%)
  matrix products  34.8 us (22%)
  waiting for transfers between devices  22.3 us (14%)
  between operations  14.1 us (9%)
  other arithmetic  7.18 us (4%)
  local copies, waits for them, and re-layouts  3.16 us (2%)
    psum x1, blocking collectives, on_device(): grad = lax.psum(jnp.sum(tile_terms, 1), ('row', 'col')) / total_rows  39.4 us
    all_gather x1, blocking collectives, on_device(): gathered = lax.all_gather(own_rows, 'col', axis=1, tiled=True)  32 us
    reduce_scatter x1, waiting for transfers between devices, on_device(): summed = lax.psum_scatter(partials, 'col', scatter_dimension=1, tiled=True)  22.2 us
    dot_general x8, matrix products, add_block(): lax.dot_general(values, kernel, (((1,), (1,)), ((), ())), precision=lax.P...  20.1 us
    dot_general x8, matrix products, add_block(): lax.dot_general(row_block, col_scaled, (((0,), (0,)), ((), ())), precisio...  14.7 us
    all_gather x1, blocking collectives, on_device(): shard_piece = lax.all_gather(own_cols, 'row', axis=1, tiled=True)  6.32 us
  transfers between devices with their start and end apart: 1, of which 1 were waited for; matrix products, arithmetic and copies ran while one was open for 2% of the time, Pallas kernels for 0%

commit v1 on v0

--- a/solution.py
+++ b/solution.py
@@ -26,7 +26,12 @@
     inverse_scale = 1.0 / lengthscale
     own_scaled = x_rows * inverse_scale[:, None]
     own_rows = jnp.concatenate([own_scaled, alpha_rows[None, :]], 0)
-    gathered = lax.all_gather(own_rows, "col", axis=1, tiled=True)
+    ring = [own_rows]
+    for hop in range(7):
+        ring.append(lax.ppermute(ring[-1], "col", [(dev, (dev + 1) % 8) for dev in range(8)]))
+    gathered = jnp.roll(
+        jnp.concatenate(ring[::-1], axis=1), (lax.axis_index("col") + 1) * ring[0].shape[1], axis=1
+    )
     row_scaled = gathered[:dims]
     row_alpha = gathered[dims]
     row_count = row_scaled.shape[1]

time: 160 us -> 167 us (1.044)
  waiting for transfers between devices: 22.3 us -> 60.2 us
  blocking collectives: 77.7 us -> 42.4 us
  starting transfers between devices: 0.04 us -> 3.05 us
    ppermute x0 -> x7, waiting for transfers between devices: none -> 39 us  [on_device(): lax.ppermute(ring[-1], 'col', [(dev, (dev + 1) % 8) for dev in range(8)])]
    all_gather x1 -> x0, blocking collectives: 32 us -> none  [on_device(): gathered = lax.all_gather(own_rows, 'col', axis=1, tiled=True)]
    ppermute x0 -> x7, starting transfers between devices: none -> 3.01 us  [on_device(): lax.ppermute(ring[-1], 'col', [(dev, (dev + 1) % 8) for dev in range(8)])]
    psum x1, blocking collectives: 39.4 us -> 37.1 us  [on_device(): grad = lax.psum(jnp.sum(tile_terms, 1), ('row', 'col')) / total_rows]
  transfers between devices with their start and end apart: 1 -> 8, of which waited for: 1 -> 8; matrix products, arithmetic and copies ran while one was open for 2% -> 3% of each run, Pallas kernels for 0% -> 0%
where the time goes in v1:
time: 167 us; the launch traced here: 166 us
  waiting for transfers between devices  60.2 us (36%)
  blocking collectives  42.4 us (25%)
  matrix products  34.9 us (21%)
  between operations  14.2 us (9%)
  other arithmetic  7.88 us (5%)
  local copies, waits for them, and re-layouts  3.24 us (2%)
  starting transfers between devices  3.05 us (2%)
    ppermute x7, waiting for transfers between devices, on_device(): lax.ppermute(ring[-1], 'col', [(dev, (dev + 1) % 8) for dev in range(8)])  39 us
    psum x1, blocking collectives, on_device(): grad = lax.psum(jnp.sum(tile_terms, 1), ('row', 'col')) / total_rows  37.1 us
    reduce_scatter x1, waiting for transfers between devices, on_device(): summed = lax.psum_scatter(partials, 'col', scatter_dimension=1, tiled=True)  21.2 us
    dot_general x8, matrix products, add_block(): lax.dot_general(values, kernel, (((1,), (1,)), ((), ())), precision=lax.P...  20.2 us
    dot_general x8, matrix products, add_block(): lax.dot_general(row_block, col_scaled, (((0,), (0,)), ((), ())), precisio...  14.7 us
    all_gather x1, blocking collectives, on_device(): shard_piece = lax.all_gather(own_cols, 'row', axis=1, tiled=True)  5.31 us
  transfers between devices with their start and end apart: 8, of which 8 were waited for; matrix products, arithmetic and copies ran while one was open for 3% of the time, Pallas kernels for 0%

profile of v1, /device:TPU:0, one launch (start us, length us, event | category | flops | bytes accessed | tf_op | source)
XLA Modules:
  0.0 166.2 jit_solution(17845357251310154505)
XLA Ops:
  7.2 0.0 copy-start.2
  7.2 0.0 reduce-scatter.2.cloned.1.call-start
  7.2 0.7 broadcast_divide_fusion
  7.9 0.8 broadcast_multiply_fusion.1
  8.7 0.7 pad_maximum_fusion.1
  9.4 3.0 %collective-permute-start = (f32[17,512]{1,0:T(8,128)S(1)}, f32[17,512]{1,0:T(8,128)S(1)}, u32[]{:S(2)}, u32[]{:S(2)}) collective-permute-start(f32[17,512]{1,0:T(8,128)S(1)} %pad_maximum_fusion.1), channel_id=1, source_target_pairs={{0,1},{1,2},{2,3},{3,4},{4,5},{5,6},{6,7},{7,0},{8,9},{9,10},{10,1... | collective-permute-start | bytes 104456 | tf_op jit(solution)/shard_map/ppermute | solution.py:31
  12.4 5.1 %collective-permute-done = f32[17,512]{1,0:T(8,128)S(1)} collective-permute-done((f32[17,512]{1,0:T(8,128)S(1)}, f32[17,512]{1,0:T(8,128)S(1)}, u32[]{:S(2)}, u32[]{:S(2)}) %collective-permute-start) | collective-permute-done | bytes 34848 | tf_op jit(solution)/shard_map/ppermute | solution.py:31
  17.5 0.0 collective-permute-start.1
  17.5 6.8 %collective-permute-done.1 = f32[17,512]{1,0:T(8,128)S(1)} collective-permute-done((f32[17,512]{1,0:T(8,128)S(1)}, f32[17,512]{1,0:T(8,128)S(1)}, u32[]{:S(2)}, u32[]{:S(2)}) %collective-permute-start.1) | collective-permute-done | bytes 34848 | tf_op jit(solution)/shard_map/ppermute | solution.py:31
  24.3 0.0 collective-permute-start.2
  24.3 6.8 %collective-permute-done.2 = f32[17,512]{1,0:T(8,128)S(1)} collective-permute-done((f32[17,512]{1,0:T(8,128)S(1)}, f32[17,512]{1,0:T(8,128)S(1)}, u32[]{:S(2)}, u32[]{:S(2)}) %collective-permute-start.2) | collective-permute-done | bytes 34848 | tf_op jit(solution)/shard_map/ppermute | solution.py:31
  31.1 0.0 collective-permute-start.3
  31.1 0.8 broadcast_multiply_fusion.2
  31.9 6.0 %collective-permute-done.3 = f32[17,512]{1,0:T(8,128)S(1)} collective-permute-done((f32[17,512]{1,0:T(8,128)S(1)}, f32[17,512]{1,0:T(8,128)S(1)}, u32[]{:S(2)}, u32[]{:S(2)}) %collective-permute-start.3) | collective-permute-done | bytes 34848 | tf_op jit(solution)/shard_map/ppermute | solution.py:31
  37.9 0.0 collective-permute-start.4
  37.9 0.7 pad_maximum_fusion.2
  38.6 5.3 %all_gather.3 = f32[17,1024]{1,0:T(8,128)S(1)} all-gather(f32[17,256]{1,0:T(8,128)S(1)} %pad_maximum_fusion.2), channel_id=1, replica_groups=mesh['row'=4,'col'=8] {'row'}, dimensions={1}, use_global_device_ids=true | all-gather | bytes 87040 | tf_op jit(solution)/shard_map/all_gather | solution.py:43
  43.9 0.8 collective-permute-done.4
  44.7 0.0 collective-permute-start.5
  44.7 6.8 %collective-permute-done.5 = f32[17,512]{1,0:T(8,128)S(1)} collective-permute-done((f32[17,512]{1,0:T(8,128)S(1)}, f32[17,512]{1,0:T(8,128)S(1)}, u32[]{:S(2)}, u32[]{:S(2)}) %collective-permute-start.5) | collective-permute-done | bytes 34848 | tf_op jit(solution)/shard_map/ppermute | solution.py:31
  51.4 0.0 collective-permute-start.6
  51.5 6.7 %collective-permute-done.6 = f32[17,512]{1,0:T(8,128)S(1)} collective-permute-done((f32[17,512]{1,0:T(8,128)S(1)}, f32[17,512]{1,0:T(8,128)S(1)}, u32[]{:S(2)}, u32[]{:S(2)}) %collective-permute-start.6) | collective-permute-done | bytes 34848 | tf_op jit(solution)/shard_map/ppermute | solution.py:31
  58.3 0.7 constant_dynamic-update-slice_fusion.8
  59.1 0.0 copy-done.2
  59.1 0.1 multiply_reduce_fusion.1
  59.2 0.0 copy-start.1
  59.2 35.8 %while.13 = (s32[]{:T(128)}, f32[33,4096]{1,0:T(8,128)S(1)}, f32[4096]{0:T(1024)S(1)}, f32[1024]{0:T(1024)S(1)}, f32[16,4096]{1,0:T(8,128)S(1)}, /*index=5*/f32[...) while((s32[]{:T(128)}, f32[33,4096]{1,0:T(8,128)S(1)}, ...), condition=%wide.region_3.4_spmd, body=%wide.region_2.3_spmd.sunk | while | flops 310395392 | bytes 4630695 | solution.py:78
  59.3 0.1 dynamic_slice.34
  59.3 1.8 %fusion.39 = f32[512,1024]{1,0:T(8,128)S(1)} fusion(f32[16,1024]{1,0:T(8,128)S(1)} %get-tuple-element.218, f32[16,4096]{1,0:T(8,128)S(1)} %get-tuple-element.217, s32[]{:T(128)S(6)} %select_n.26), kind=kOutput, calls=%fused_computation.13.clone.1 | convolution fusion | flops 100663296 | bytes 2195460 | tf_op jit(solution)/shard_map/while/body/eval_jaxpr/dot_general | solution.py:60
  61.2 2.5 %fusion.40 = f32[33,4096]{1,0:T(8,128)S(1)} fusion(f32[33,4096]{1,0:T(8,128)S(1)} %get-tuple-element.203, s32[]{:T(128)S(6)} %select_n.26, f32[33,1024]{1,0:T(8,128)S(1)} %get-tuple-element.219, f32[512,1024]{1,0:T(8,128)S(1)} %fusion.39, f32[1024]{0:T(1024)S(1)} %get-tuple-element.216, f32[512]{0:T(512)S(1)} %dynamic_slice.34), kind=kOutput, calls=%fused_computation.8.clone.1 | convolution fusion | flops 209732096 | bytes 2430980 | tf_op jit(solution)/shard_map/while/body/eval_jaxpr/dot_general | solution.py:68
  63.7 0.1 dynamic_slice.34
  63.8 1.8 %fusion.39 = f32[512,1024]{1,0:T(8,128)S(1)} fusion(f32[16,1024]{1,0:T(8,128)S(1)} %get-tuple-element.218, f32[16,4096]{1,0:T(8,128)S(1)} %get-tuple-element.217, s32[]{:T(128)S(6)} %select_n.26), kind=kOutput, calls=%fused_computation.13.clone.1 | convolution fusion | flops 100663296 | bytes 2195460 | tf_op jit(solution)/shard_map/while/body/eval_jaxpr/dot_general | solution.py:60
  65.7 2.5 %fusion.40 = f32[33,4096]{1,0:T(8,128)S(1)} fusion(f32[33,4096]{1,0:T(8,128)S(1)} %get-tuple-element.203, s32[]{:T(128)S(6)} %select_n.26, f32[33,1024]{1,0:T(8,128)S(1)} %get-tuple-element.219, f32[512,1024]{1,0:T(8,128)S(1)} %fusion.39, f32[1024]{0:T(1024)S(1)} %get-tuple-element.216, f32[512]{0:T(512)S(1)} %dynamic_slice.34), kind=kOutput, calls=%fused_computation.8.clone.1 | convolution fusion | flops 209732096 | bytes 2430980 | tf_op jit(solution)/shard_map/while/body/eval_jaxpr/dot_general | solution.py:68
  68.2 0.1 dynamic_slice.34
  68.3 1.8 %fusion.39 = f32[512,1024]{1,0:T(8,128)S(1)} fusion(f32[16,1024]{1,0:T(8,128)S(1)} %get-tuple-element.218, f32[16,4096]{1,0:T(8,128)S(1)} %get-tuple-element.217, s32[]{:T(128)S(6)} %select_n.26), kind=kOutput, calls=%fused_computation.13.clone.1 | convolution fusion | flops 100663296 | bytes 2195460 | tf_op jit(solution)/shard_map/while/body/eval_jaxpr/dot_general | solution.py:60
  70.1 2.5 %fusion.40 = f32[33,4096]{1,0:T(8,128)S(1)} fusion(f32[33,4096]{1,0:T(8,128)S(1)} %get-tuple-element.203, s32[]{:T(128)S(6)} %select_n.26, f32[33,1024]{1,0:T(8,128)S(1)} %get-tuple-element.219, f32[512,1024]{1,0:T(8,128)S(1)} %fusion.39, f32[1024]{0:T(1024)S(1)} %get-tuple-element.216, f32[512]{0:T(512)S(1)} %dynamic_slice.34), kind=kOutput, calls=%fused_computation.8.clone.1 | convolution fusion | flops 209732096 | bytes 2430980 | tf_op jit(solution)/shard_map/while/body/eval_jaxpr/dot_general | solution.py:68
  72.7 0.1 dynamic_slice.34
  72.8 1.8 %fusion.39 = f32[512,1024]{1,0:T(8,128)S(1)} fusion(f32[16,1024]{1,0:T(8,128)S(1)} %get-tuple-element.218, f32[16,4096]{1,0:T(8,128)S(1)} %get-tuple-element.217, s32[]{:T(128)S(6)} %select_n.26), kind=kOutput, calls=%fused_computation.13.clone.1 | convolution fusion | flops 100663296 | bytes 2195460 | tf_op jit(solution)/shard_map/while/body/eval_jaxpr/dot_general | solution.py:60
  74.6 2.5 %fusion.40 = f32[33,4096]{1,0:T(8,128)S(1)} fusion(f32[33,4096]{1,0:T(8,128)S(1)} %get-tuple-element.203, s32[]{:T(128)S(6)} %select_n.26, f32[33,1024]{1,0:T(8,128)S(1)} %get-tuple-element.219, f32[512,1024]{1,0:T(8,128)S(1)} %fusion.39, f32[1024]{0:T(1024)S(1)} %get-tuple-element.216, f32[512]{0:T(512)S(1)} %dynamic_slice.34), kind=kOutput, calls=%fused_computation.8.clone.1 | convolution fusion | flops 209732096 | bytes 2430980 | tf_op jit(solution)/shard_map/while/body/eval_jaxpr/dot_general | solution.py:68
  77.2 0.1 dynamic_slice.34
  77.2 1.8 %fusion.39 = f32[512,1024]{1,0:T(8,128)S(1)} fusion(f32[16,1024]{1,0:T(8,128)S(1)} %get-tuple-element.218, f32[16,4096]{1,0:T(8,128)S(1)} %get-tuple-element.217, s32[]{:T(128)S(6)} %select_n.26), kind=kOutput, calls=%fused_computation.13.clone.1 | convolution fusion | flops 100663296 | bytes 2195460 | tf_op jit(solution)/shard_map/while/body/eval_jaxpr/dot_general | solution.py:60
  79.1 2.5 %fusion.40 = f32[33,4096]{1,0:T(8,128)S(1)} fusion(f32[33,4096]{1,0:T(8,128)S(1)} %get-tuple-element.203, s32[]{:T(128)S(6)} %select_n.26, f32[33,1024]{1,0:T(8,128)S(1)} %get-tuple-element.219, f32[512,1024]{1,0:T(8,128)S(1)} %fusion.39, f32[1024]{0:T(1024)S(1)} %get-tuple-element.216, f32[512]{0:T(512)S(1)} %dynamic_slice.34), kind=kOutput, calls=%fused_computation.8.clone.1 | convolution fusion | flops 209732096 | bytes 2430980 | tf_op jit(solution)/shard_map/while/body/eval_jaxpr/dot_general | solution.py:68
  81.6 0.1 dynamic_slice.34
  81.7 1.8 %fusion.39 = f32[512,1024]{1,0:T(8,128)S(1)} fusion(f32[16,1024]{1,0:T(8,128)S(1)} %get-tuple-element.218, f32[16,4096]{1,0:T(8,128)S(1)} %get-tuple-element.217, s32[]{:T(128)S(6)} %select_n.26), kind=kOutput, calls=%fused_computation.13.clone.1 | convolution fusion | flops 100663296 | bytes 2195460 | tf_op jit(solution)/shard_map/while/body/eval_jaxpr/dot_general | solution.py:60
  83.5 2.5 %fusion.40 = f32[33,4096]{1,0:T(8,128)S(1)} fusion(f32[33,4096]{1,0:T(8,128)S(1)} %get-tuple-element.203, s32[]{:T(128)S(6)} %select_n.26, f32[33,1024]{1,0:T(8,128)S(1)} %get-tuple-element.219, f32[512,1024]{1,0:T(8,128)S(1)} %fusion.39, f32[1024]{0:T(1024)S(1)} %get-tuple-element.216, f32[512]{0:T(512)S(1)} %dynamic_slice.34), kind=kOutput, calls=%fused_computation.8.clone.1 | convolution fusion | flops 209732096 | bytes 2430980 | tf_op jit(solution)/shard_map/while/body/eval_jaxpr/dot_general | solution.py:68
  86.1 0.1 dynamic_slice.34
  86.2 1.8 %fusion.39 = f32[512,1024]{1,0:T(8,128)S(1)} fusion(f32[16,1024]{1,0:T(8,128)S(1)} %get-tuple-element.218, f32[16,4096]{1,0:T(8,128)S(1)} %get-tuple-element.217, s32[]{:T(128)S(6)} %select_n.26), kind=kOutput, calls=%fused_computation.13.clone.1 | convolution fusion | flops 100663296 | bytes 2195460 | tf_op jit(solution)/shard_map/while/body/eval_jaxpr/dot_general | solution.py:60
  88.0 2.5 %fusion.40 = f32[33,4096]{1,0:T(8,128)S(1)} fusion(f32[33,4096]{1,0:T(8,128)S(1)} %get-tuple-element.203, s32[]{:T(128)S(6)} %select_n.26, f32[33,1024]{1,0:T(8,128)S(1)} %get-tuple-element.219, f32[512,1024]{1,0:T(8,128)S(1)} %fusion.39, f32[1024]{0:T(1024)S(1)} %get-tuple-element.216, f32[512]{0:T(512)S(1)} %dynamic_slice.34), kind=kOutput, calls=%fused_computation.8.clone.1 | convolution fusion | flops 209732096 | bytes 2430980 | tf_op jit(solution)/shard_map/while/body/eval_jaxpr/dot_general | solution.py:68
  90.6 0.1 dynamic_slice.34
  90.6 1.8 %fusion.39 = f32[512,1024]{1,0:T(8,128)S(1)} fusion(f32[16,1024]{1,0:T(8,128)S(1)} %get-tuple-element.218, f32[16,4096]{1,0:T(8,128)S(1)} %get-tuple-element.217, s32[]{:T(128)S(6)} %select_n.26), kind=kOutput, calls=%fused_computation.13.clone.1 | convolution fusion | flops 100663296 | bytes 2195460 | tf_op jit(solution)/shard_map/while/body/eval_jaxpr/dot_general | solution.py:60
  92.5 2.5 %fusion.40 = f32[33,4096]{1,0:T(8,128)S(1)} fusion(f32[33,4096]{1,0:T(8,128)S(1)} %get-tuple-element.203, s32[]{:T(128)S(6)} %select_n.26, f32[33,1024]{1,0:T(8,128)S(1)} %get-tuple-element.219, f32[512,1024]{1,0:T(8,128)S(1)} %fusion.39, f32[1024]{0:T(1024)S(1)} %get-tuple-element.216, f32[512]{0:T(512)S(1)} %dynamic_slice.34), kind=kOutput, calls=%fused_computation.8.clone.1 | convolution fusion | flops 209732096 | bytes 2430980 | tf_op jit(solution)/shard_map/while/body/eval_jaxpr/dot_general | solution.py:68
  95.0 0.0 copy-start
  95.0 0.8 copy-done
  95.9 0.0 reduce-scatter.2.cloned.1.call-update
  95.9 0.9 slice.37
  96.8 1.3 multiply_reduce_fusion
  98.2 37.1 %psum.7 = f32[16]{0:T(128)S(1)} all-reduce(f32[16]{0:T(128)S(1)} %multiply_reduce_fusion), channel_id=1, replica_groups=mesh['row'=4,'col'=8] {'row','col'}, use_global_device_ids=true, to_apply=%region_6.7 | all-reduce | flops 16 | bytes 128 | tf_op jit(solution)/shard_map/psum | solution.py:83
  135.3 0.5 broadcast_multiply_fusion.4
  135.8 21.2 %reduce-scatter.2.cloned.1.call-done = f32[33,512]{1,0:T(8,128)} async-done(((f32[33,4096]{1,0:T(8,128)}), f32[33,512]{1,0:T(8,128)}) %reduce-scatter.2.cloned.1.call-update) | async-done | bytes 67600 | tf_op jit(solution)/shard_map/reduce_scatter | solution.py:79
  157.0 0.7 slice.42
  157.8 0.0 copy-start.3
  157.8 0.0 copy-done.1
  157.8 1.6 fusion.24
  159.3 0.0 copy-done.3
  (21 shorter events, 0.2 us)
Async XLA Ops:
  7.2 51.9 %copy-start.2 = (f32[512]{0:T(512)S(1)}, f32[512]{0:T(512)}, u32[]{:S(2)}) copy-start(f32[512]{0:T(512)} %param.8) | copy-start | bytes 6148
  7.2 149.9 %reduce-scatter.2.cloned.1.call-start = ((), (), s32[]{:S(2)}) async-start(), calls=%async_computation.1 | async-start | bytes 737280 | tf_op jit(solution)/shard_map/reduce_scatter | solution.py:79
  9.4 8.1 %collective-permute-start = (f32[17,512]{1,0:T(8,128)S(1)}, f32[17,512]{1,0:T(8,128)S(1)}, u32[]{:S(2)}, u32[]{:S(2)}) collective-permute-start(f32[17,512]{1,0:T(8,128)S(1)} %pad_maximum_fusion.1), channel_id=1, source_target_pairs={{0,1},{1,2},{2,3},{3,4},{4,5},{5,6},{6,7},{7,0},{8,9},{9,10},{10,1... | collective-permute-start | bytes 104456 | tf_op jit(solution)/shard_map/ppermute | solution.py:31
  17.5 6.8 %collective-permute-start.1 = (f32[17,512]{1,0:T(8,128)S(1)}, f32[17,512]{1,0:T(8,128)S(1)}, u32[]{:S(2)}, u32[]{:S(2)}) collective-permute-start(f32[17,512]{1,0:T(8,128)S(1)} %collective-permute-done), channel_id=1, source_target_pairs={{0,1},{1,2},{2,3},{3,4},{4,5},{5,6},{6,7},{7,0},{8,9},{9,10},{10,1... | collective-permute-start | bytes 104456 | tf_op jit(solution)/shard_map/ppermute | solution.py:31
  24.3 6.8 %collective-permute-start.2 = (f32[17,512]{1,0:T(8,128)S(1)}, f32[17,512]{1,0:T(8,128)S(1)}, u32[]{:S(2)}, u32[]{:S(2)}) collective-permute-start(f32[17,512]{1,0:T(8,128)S(1)} %collective-permute-done.1), channel_id=1, source_target_pairs={{0,1},{1,2},{2,3},{3,4},{4,5},{5,6},{6,7},{7,0},{8,9},{9,10},{10,1... | collective-permute-start | bytes 104456 | tf_op jit(solution)/shard_map/ppermute | solution.py:31
  31.1 6.8 %collective-permute-start.3 = (f32[17,512]{1,0:T(8,128)S(1)}, f32[17,512]{1,0:T(8,128)S(1)}, u32[]{:S(2)}, u32[]{:S(2)}) collective-permute-start(f32[17,512]{1,0:T(8,128)S(1)} %collective-permute-done.2), channel_id=1, source_target_pairs={{0,1},{1,2},{2,3},{3,4},{4,5},{5,6},{6,7},{7,0},{8,9},{9,10},{10,1... | collective-permute-start | bytes 104456 | tf_op jit(solution)/shard_map/ppermute | solution.py:31
  37.9 6.8 %collective-permute-start.4 = (f32[17,512]{1,0:T(8,128)S(1)}, f32[17,512]{1,0:T(8,128)S(1)}, u32[]{:S(2)}, u32[]{:S(2)}) collective-permute-start(f32[17,512]{1,0:T(8,128)S(1)} %collective-permute-done.3), channel_id=1, source_target_pairs={{0,1},{1,2},{2,3},{3,4},{4,5},{5,6},{6,7},{7,0},{8,9},{9,10},{10,1... | collective-permute-start | bytes 104456 | tf_op jit(solution)/shard_map/ppermute | solution.py:31
  44.7 6.8 %collective-permute-start.5 = (f32[17,512]{1,0:T(8,128)S(1)}, f32[17,512]{1,0:T(8,128)S(1)}, u32[]{:S(2)}, u32[]{:S(2)}) collective-permute-start(f32[17,512]{1,0:T(8,128)S(1)} %collective-permute-done.4), channel_id=1, source_target_pairs={{0,1},{1,2},{2,3},{3,4},{4,5},{5,6},{6,7},{7,0},{8,9},{9,10},{10,1... | collective-permute-start | bytes 104456 | tf_op jit(solution)/shard_map/ppermute | solution.py:31
  51.4 6.8 %collective-permute-start.6 = (f32[17,512]{1,0:T(8,128)S(1)}, f32[17,512]{1,0:T(8,128)S(1)}, u32[]{:S(2)}, u32[]{:S(2)}) collective-permute-start(f32[17,512]{1,0:T(8,128)S(1)} %collective-permute-done.5), channel_id=1, source_target_pairs={{0,1},{1,2},{2,3},{3,4},{4,5},{5,6},{6,7},{7,0},{8,9},{9,10},{10,1... | collective-permute-start | bytes 104456 | tf_op jit(solution)/shard_map/ppermute | solution.py:31
  59.2 98.5 %copy-start.1 = (f32[16,512]{1,0:T(8,128)S(1)}, f32[16,512]{1,0:T(8,128)}, u32[]{:S(2)}) copy-start(f32[16,512]{1,0:T(8,128)} %param.7) | copy-start | bytes 98308
  95.0 0.8 copy-start
  157.8 1.6 copy-start.3
Sparse Core Ops, SparseCore 0:
  96.0 60.9 reduce-scatter.1
